TPU v7x, 32 devices: a whole 2x2x4 slice. The times are simulated.
32 devices in a mesh: row: 4 (over x, core), col: 8 (over z, y).
Axes of the slice: x: 2, y: 2, z: 4, core: 2. Of those that a mesh axis runs over, the one named last changes fastest.
Arguments:
- images: bfloat16 [128, 28, 28, 512], P(('row', 'col')), may hold values from -30 to 30
- w_reduce: bfloat16 [2, 512, 128], replicated, may hold values from -0.25 to 0.25
- w_spatial: bfloat16 [2, 3, 3, 128, 128], replicated, may hold values from -0.1875 to 0.1875
- w_expand: bfloat16 [2, 128, 512], replicated, may hold values from -0.5 to 0.5
- gain_mid: float32 [2, 2, 128], replicated, may hold values from 0.5 to 1.5
- bias_mid: float32 [2, 2, 128], replicated, may hold values from -3 to 3
- mean_mid: float32 [2, 2, 128], replicated, may hold values from -2 to 2
- var_mid: float32 [2, 2, 128], replicated, may hold values from 0.05 to 20
- gain_out: float32 [2, 512], replicated, may hold values from 0.5 to 1.5
- bias_out: float32 [2, 512], replicated, may hold values from -3 to 3
- mean_out: float32 [2, 512], replicated, may hold values from -2 to 2
- var_out: float32 [2, 512], replicated, may hold values from 0.05 to 20
Outputs:
- features: bfloat16 [128, 28, 28, 512], P(('row', 'col'))
All inputs are finite; a program needn't handle non-finite values.
Results may differ from a plain program's by a relative error of at most 0.0075.
Values sent between devices are 32-bit elements; how exact they have to be, the bound alone decides.
A program may use at most 64 MiB of HBM per device.

v0:
```python
import functools

import jax
import jax.numpy as jnp
from jax import lax
from jax.experimental import pallas as pl
from jax.experimental.pallas import tpu as pltpu
from jax.sharding import PartitionSpec as P

epsilon = 1e-05
ratio_max = 3.0
shift_max = 5.0
MESH = pl.DeviceIdType.MESH
LANES = 128
f32 = jnp.float32
bf16 = jnp.bfloat16


def coefficients(total, gain, bias, run_mean, run_var, count):
    mean_offset = total[0:1] / count
    center = run_mean + mean_offset
    variance = jnp.maximum(total[1:2] / count - mean_offset * mean_offset, 0.0)
    sigma = jnp.sqrt(variance + epsilon)
    run_sigma = jnp.sqrt(run_var + epsilon)
    ratio = jnp.clip(sigma / run_sigma, 1.0 / ratio_max, ratio_max)
    shift = jnp.clip(mean_offset / run_sigma, -shift_max, shift_max)
    return center, gain * (ratio / sigma), gain * shift + bias


def main_kernel(
    rows,
    cols,
    count,
    side,
    tiles,
    img_ref,
    wr_hbm,
    ws_hbm,
    we_hbm,
    gm_hbm,
    bm_hbm,
    mm_hbm,
    vm_hbm,
    go_hbm,
    bo_hbm,
    mo_hbm,
    vo_hbm,
    x4_ref,
    z3_ref,
    coef_ref,
    z_ref,
    hc_ref,
    w2_ref,
    mid_buf,
    out_buf,
    wr_ref,
    we_ref,
    gm_ref,
    bm_ref,
    mm_ref,
    vm_ref,
    go_ref,
    bo_ref,
    mo_ref,
    vo_ref,
    in_sem,
    par_sem,
    tap_sem,
    send_sem,
    recv_sem,
):
    devices = rows * cols
    pixels, images, channels = img_ref.shape
    blocks, _, middle = wr_ref.shape
    slabs = channels // LANES
    line = side * images
    tall = side // tiles
    part = tall * line
    my_row, my_col = lax.axis_index("row"), lax.axis_index("col")
    me = my_row * cols + my_col
    x_ref = x4_ref.reshape(slabs, pixels * images, LANES)

    def slab_copy(t, c):
        span = pl.ds(t * (pixels // tiles), pixels // tiles)
        far = img_ref.at[span, :, pl.ds(c * LANES, LANES)]
        return pltpu.make_async_copy(far, x4_ref.at[c, span], in_sem.at[t, c])

    pairs = (
        (wr_hbm, wr_ref), (mm_hbm, mm_ref), (we_hbm, we_ref), (gm_hbm, gm_ref),
        (bm_hbm, bm_ref), (vm_hbm, vm_ref), (go_hbm, go_ref), (bo_hbm, bo_ref),
        (mo_hbm, mo_ref), (vo_hbm, vo_ref),
    )
    loads = [pltpu.make_async_copy(a, b, par_sem.at[i]) for i, (a, b) in enumerate(pairs)]
    kernels = [
        pltpu.make_async_copy(
            ws_hbm.at[block],
            w2_ref.at[block, pl.ds(3 * i * middle, 9 * middle), pl.ds(i * middle, middle)],
            tap_sem.at[block, i],
        )
        for block in range(blocks)
        for i in range(2)
    ]
    for copy in loads[:2]:
        copy.start()
    for t in range(tiles):
        for c in range(slabs):
            slab_copy(t, c).start()
    for copy in loads[2:] + kernels:
        copy.start()

    barrier = pltpu.get_barrier_semaphore()

    def to_all(act):
        if devices <= 64:
            far_rows = [lax.rem(my_row + i, rows) for i in range(rows)]
            far_cols = [lax.rem(my_col + i, cols) for i in range(cols)]
            for j in range(cols - 1, -1, -1):
                for i in range(rows):
                    if i or j:
                        act((far_rows[i], far_cols[j]))
        else:

            def step(i, c):
                other = lax.rem(me + i, devices)
                act((lax.div(other, cols), lax.rem(other, cols)))
                return c

            lax.fori_loop(1, devices, step, 0)

    to_all(
        lambda there: pl.semaphore_signal(
            barrier, inc=1, device_id=there, device_id_type=MESH
        )
    )

    def exchange(buf, slot, sums, gain, bias, mean, var, index, first):
        for i in range(2):
            buf[slot, me, pl.ds(i, 1), :] = jnp.sum(sums[i], axis=0, keepdims=True)
        if first:
            pl.semaphore_wait(barrier, devices - 1)

        def send(there):
            pltpu.make_async_remote_copy(
                src_ref=buf.at[slot, me],
                dst_ref=buf.at[slot, me],
                send_sem=send_sem.at[index],
                recv_sem=recv_sem.at[index],
                device_id=there,
                device_id_type=MESH,
            ).start()

        to_all(send)
        others = buf.at[slot, pl.ds(0, devices - 1)]
        whole = pltpu.make_async_remote_copy(
            src_ref=others,
            dst_ref=others,
            send_sem=send_sem.at[index],
            recv_sem=recv_sem.at[index],
            device_id=(lax.rem(my_row + 1, rows), my_col),
            device_id_type=MESH,
        )
        whole.wait_send()
        whole.wait_recv()
        total = jnp.sum(buf[slot], axis=0)
        return coefficients(total, gain, bias, mean, var, count)

    def moments(z, mean, sums):
        d = (z - mean).reshape(-1, 16, z.shape[-1])
        return sums[0] + jnp.sum(d, axis=0), sums[1] + jnp.sum(d * d, axis=0)

    def zeros(c):
        return (jnp.zeros((16, c), f32), jnp.zeros((16, c), f32))

    hc_ref[0] = jnp.zeros((line, 3 * middle), bf16)
    hc_ref[side + 1] = jnp.zeros((line, 3 * middle), bf16)
    empty = jnp.zeros((3 * middle, middle), bf16)
    for block in range(blocks):
        w2_ref[block, pl.ds(9 * middle, 3 * middle), 0:middle] = empty
        w2_ref[block, pl.ds(0, 3 * middle), middle : 2 * middle] = empty
    for copy in loads[:2]:
        copy.wait()
    place = lax.broadcasted_iota(jnp.int32, (1, line, 1), 1)

    def updated(t, coef):
        center, scale, offset = coef
        span = pl.ds(pl.multiple_of(t * part, 16), part)
        new = []
        for c in range(slabs):
            lanes = slice(c * LANES, (c + 1) * LANES)
            z = (z3_ref[span, lanes] - center[:, lanes]) * scale[:, lanes] + offset[:, lanes]
            y = jnp.maximum(z + x_ref[c, span, :].astype(f32), 0.0).astype(bf16)
            x_ref[c, span, :] = y
            new.append(y)
        return new

    out_coef = None
    for block in range(blocks):
        mean_one = mm_ref[block, pl.ds(0, 1), :]
        mean_two = mm_ref[block, pl.ds(1, 1), :]

        def reduce_step(t, sums):
            if block == 0:
                for c in range(slabs):
                    slab_copy(t, c).wait()
                span = pl.ds(pl.multiple_of(t * part, 16), part)
                x = [x_ref[c, span, :] for c in range(slabs)]
            else:
                x = updated(t, out_coef)
            x = jnp.concatenate(x, axis=1)
            z = jnp.dot(x, wr_ref[block], preferred_element_type=f32)
            z_ref[t] = z.reshape(tall // 2, 2, line, middle)
            return moments(z, mean_one, sums)

        sums = lax.fori_loop(0, tiles, reduce_step, zeros(middle), unroll=True)
        if block == 0:
            for copy in loads[2:] + kernels:
                copy.wait()
        mean_out = mo_ref[pl.ds(block, 1), :]
        center1, scale1, offset1 = exchange(
            mid_buf, 2 * block, sums,
            gm_ref[block, pl.ds(0, 1), :], bm_ref[block, pl.ds(0, 1), :],
            mean_one, vm_ref[block, pl.ds(0, 1), :], 3 * block, block == 0,
        )

        def taps_step(t, carry):
            z = z_ref[t].reshape(part, middle)
            h = jnp.maximum((z - center1) * scale1 + offset1, 0.0)
            left = pltpu.roll(h, images, 0).reshape(tall, line, middle)
            right = pltpu.roll(h, part - images, 0).reshape(tall, line, middle)
            left = jnp.where(place >= images, left, 0.0)
            right = jnp.where(place < line - images, right, 0.0)
            taps = (left, h.reshape(tall, line, middle), right)
            for i, tap in enumerate(taps):
                lanes = slice(i * middle, (i + 1) * middle)
                hc_ref[pl.ds(t * tall + 1, tall), :, lanes] = tap.astype(bf16)
            return carry

        def conv_step(t, sums):
            v = hc_ref[pl.ds(t * tall, tall + 2)].reshape(tall // 2 + 1, 2, line, 3 * middle)
            lhs = jnp.concatenate(
                [v[:-1, 0], v[:-1, 1], v[1:, 0], v[1:, 1]], axis=-1
            ).reshape(part // 2, 12 * middle)
            z = jnp.dot(lhs, w2_ref[block], preferred_element_type=f32)
            for i in range(2):
                half = z[:, i * middle : (i + 1) * middle]
                z_ref[t, :, i] = half.reshape(tall // 2, line, middle)
                sums = moments(half, mean_two, sums)
            return sums

        lax.fori_loop(0, tiles, taps_step, 0, unroll=True)
        sums = lax.fori_loop(0, tiles, conv_step, zeros(middle), unroll=True)
        center2, scale2, offset2 = exchange(
            mid_buf, 2 * block + 1, sums,
            gm_ref[block, pl.ds(1, 1), :], bm_ref[block, pl.ds(1, 1), :],
            mean_two, vm_ref[block, pl.ds(1, 1), :], 3 * block + 1, False,
        )

        def expand_step(t, sums):
            z = z_ref[t].reshape(part, middle)
            h = jnp.maximum((z - center2) * scale2 + offset2, 0.0).astype(bf16)
            z = jnp.dot(h, we_ref[block], preferred_element_type=f32)
            z3_ref[pl.ds(pl.multiple_of(t * part, 16), part), :] = z
            return moments(z, mean_out, sums)

        sums = lax.fori_loop(0, tiles, expand_step, zeros(channels), unroll=True)
        out_coef = exchange(
            out_buf, block, sums,
            go_ref[pl.ds(block, 1), :], bo_ref[pl.ds(block, 1), :],
            mean_out, vo_ref[pl.ds(block, 1), :], 3 * block + 2, False,
        )

    for i in range(3):
        coef_ref[pl.ds(i, 1), :] = out_coef[i]


def last_kernel(pieces, x4_ref, z3_ref, coef_ref, o_ref, y4_ref, out_sem):
    slabs, pixels, images, _ = x4_ref.shape
    few = pixels // pieces
    part = few * images
    x_ref = x4_ref.reshape(slabs, pixels * images, LANES)
    y_ref = y4_ref.reshape(slabs, pixels * images, LANES)

    def slab_copy(t, c):
        span = pl.ds(t * few, few)
        far = o_ref.at[span, :, pl.ds(c * LANES, LANES)]
        return pltpu.make_async_copy(y4_ref.at[c, span], far, out_sem.at[t, c])

    def step(t, carry):
        span = pl.ds(pl.multiple_of(t * part, 16), part)
        for c in range(slabs):
            lanes = slice(c * LANES, (c + 1) * LANES)
            center, scale, offset = (coef_ref[pl.ds(i, 1), lanes] for i in range(3))
            z = (z3_ref[span, lanes] - center) * scale + offset
            y = jnp.maximum(z + x_ref[c, span, :].astype(f32), 0.0)
            y_ref[c, span, :] = y.astype(bf16)
            slab_copy(t, c).start()
        return carry

    lax.fori_loop(0, pieces, step, 0)
    for t in range(pieces):
        for c in range(slabs):
            slab_copy(t, c).wait()


def local(mesh_rows, mesh_cols, images, w_reduce, w_spatial, w_expand, *params):
    held, side, _, channels = images.shape
    blocks, _, middle = w_reduce.shape
    devices = mesh_rows * mesh_cols
    count = float(held * side * side * devices)
    tiles = next(t for t in (TILES, 2, 1) if side % (2 * t) == 0)
    slabs = channels // LANES
    pixels = side * side
    vmem = pl.BlockSpec(memory_space=pltpu.VMEM)
    anywhere = pl.BlockSpec(memory_space=pltpu.HBM)
    turned = images.transpose(1, 2, 0, 3).reshape(pixels, held, channels)
    taps = w_spatial.reshape(blocks, 9 * middle, middle)
    operands = [
        pltpu.with_memory_space_constraint(a, pltpu.HBM)
        for a in (turned, w_reduce, taps, w_expand, *params)
    ]
    x4, z3, coef = pl.pallas_call(
        functools.partial(main_kernel, mesh_rows, mesh_cols, count, side, tiles),
        out_shape=(
            jax.ShapeDtypeStruct((slabs, pixels, held, LANES), bf16),
            jax.ShapeDtypeStruct((pixels * held, channels), f32),
            jax.ShapeDtypeStruct((3, channels), f32),
        ),
        in_specs=[anywhere] * 12,
        out_specs=(vmem, vmem, vmem),
        scratch_shapes=[
            pltpu.VMEM((tiles, side // tiles // 2, 2, side * held, middle), f32),
            pltpu.VMEM((side + 2, side * held, 3 * middle), bf16),
            pltpu.VMEM((blocks, 12 * middle, 2 * middle), bf16),
            pltpu.VMEM((2 * blocks, devices, 2, middle), f32),
            pltpu.VMEM((blocks, devices, 2, channels), f32),
            pltpu.VMEM(w_reduce.shape, bf16),
            pltpu.VMEM(w_expand.shape, bf16),
            *(pltpu.VMEM(p.shape, f32) for p in params),
            pltpu.SemaphoreType.DMA((tiles, slabs)),
            pltpu.SemaphoreType.DMA((10,)),
            pltpu.SemaphoreType.DMA((blocks, 2)),
            pltpu.SemaphoreType.DMA((3 * blocks,)),
            pltpu.SemaphoreType.DMA((3 * blocks,)),
        ],
        compiler_params=pltpu.CompilerParams(
            collective_id=0, has_side_effects=True, vmem_limit_bytes=LIMIT * 1024 * 1024
        ),
        name="bottlenecks",
    )(*operands)
    pieces = side // 4 if side % 4 == 0 else 1
    out = pl.pallas_call(
        functools.partial(last_kernel, pieces),
        out_shape=jax.ShapeDtypeStruct((pixels, held, channels), bf16),
        in_specs=[vmem] * 3,
        out_specs=anywhere,
        scratch_shapes=[
            pltpu.VMEM((slabs, pixels, held, LANES), bf16),
            pltpu.SemaphoreType.DMA((pieces, slabs)),
        ],
        compiler_params=pltpu.CompilerParams(vmem_limit_bytes=16 * 1024 * 1024),
        name="finish",
    )(x4, z3, coef)
    return out.reshape(side, side, held, channels).transpose(2, 0, 1, 3)


TILES = 2
LIMIT = 32


def solution(mesh):
    spec = P(("row", "col"), None, None, None)
    return jax.shard_map(
        functools.partial(local, mesh.shape["row"], mesh.shape["col"]),
        mesh=mesh,
        in_specs=(spec,) + (P(),) * 11,
        out_specs=spec,
        check_vma=False,
    )
```

profile of v0, /device:TPU:0, one launch (start us, length us, event | category | flops | bytes accessed | tf_op | source)
XLA Modules:
  0.0 48.2 jit_solution(4254364786073103183)
XLA Ops:
  0.0 45.0 %bottlenecks.1 = (bf16[4,784,4,128]{3,2,1,0:T(4,128)(2,1)S(1)}, f32[3136,512]{1,0:T(8,128)S(1)}, f32[3,512]{1,0:T(4,128)S(1)}) custom-call(bf16[784,4,512]{2,1,0:T(4,128)(2,1)} %bitcast.7, bf16[2,512,128]{2,1,0:T(8,128)(2,1)} %wr_hbm.1, bf16[2,1152,128]{2,1,0:T(8,128)(2,1)} %bitcast.8, bf16[2,128,512]{2,1,0:T(8,128)(2,1)} %we_hbm.1, f32[2,2,128]{2,1,0:T(2,128)} %gm_hbm.1, ...), custom_call_target="tpu_custom_call" | custom-call | tf_op jit(solution)/shard_map/bottlenecks/pallas_call | solution.py:321
  45.0 3.2 %finish.1 = bf16[784,4,512]{2,1,0:T(4,128)(2,1)} custom-call(bf16[4,784,4,128]{3,2,1,0:T(4,128)(2,1)S(1)} %get-tuple-element.8.x4_ref, f32[3136,512]{1,0:T(8,128)S(1)} %get-tuple-element.9.z3_ref, f32[3,512]{1,0:T(4,128)S(1)} %get-tuple-element.10.coef_ref), custom_call_target="tpu_custom_call" | custom-call | tf_op jit(solution)/shard_map/finish/pallas_call | solution.py:351
where the time goes:
time: 48.4 us; the launch traced here: 48.2 us
  Pallas kernels  48.2 us (100%)
    pallas_call x1, Pallas kernels, local(): pl.pallas_call(functools.partial(main_kernel, mesh_rows, mesh_cols, count...  45 us
    pallas_call x1, Pallas kernels, local(): pl.pallas_call(functools.partial(last_kernel, pieces), out_shape=jax.Shap...  3.22 us

commit v1 on v0

--- a/solution.py
+++ b/solution.py
@@ -45,7 +45,7 @@
     bo_hbm,
     mo_hbm,
     vo_hbm,
-    x4_ref,
+    x_ref,
     z3_ref,
     coef_ref,
     z_ref,
@@ -78,12 +78,12 @@
     part = tall * line
     my_row, my_col = lax.axis_index("row"), lax.axis_index("col")
     me = my_row * cols + my_col
-    x_ref = x4_ref.reshape(slabs, pixels * images, LANES)
+    flat_ref = img_ref.reshape(pixels * images, channels)
 
     def slab_copy(t, c):
-        span = pl.ds(t * (pixels // tiles), pixels // tiles)
-        far = img_ref.at[span, :, pl.ds(c * LANES, LANES)]
-        return pltpu.make_async_copy(far, x4_ref.at[c, span], in_sem.at[t, c])
+        span = pl.ds(t * part, part)
+        far = flat_ref.at[span, pl.ds(c * LANES, LANES)]
+        return pltpu.make_async_copy(far, x_ref.at[c, span], in_sem.at[t, c])
 
     pairs = (
         (wr_hbm, wr_ref), (mm_hbm, mm_ref), (we_hbm, we_ref), (gm_hbm, gm_ref),
@@ -273,17 +273,16 @@
         coef_ref[pl.ds(i, 1), :] = out_coef[i]
 
 
-def last_kernel(pieces, x4_ref, z3_ref, coef_ref, o_ref, y4_ref, out_sem):
-    slabs, pixels, images, _ = x4_ref.shape
-    few = pixels // pieces
-    part = few * images
-    x_ref = x4_ref.reshape(slabs, pixels * images, LANES)
-    y_ref = y4_ref.reshape(slabs, pixels * images, LANES)
+def last_kernel(pieces, x_ref, z3_ref, coef_ref, o_ref, y_ref, out_sem):
+    slabs = x_ref.shape[0]
+    pixels, images, channels = o_ref.shape
+    part = pixels // pieces * images
+    flat_ref = o_ref.reshape(pixels * images, channels)
 
     def slab_copy(t, c):
-        span = pl.ds(t * few, few)
-        far = o_ref.at[span, :, pl.ds(c * LANES, LANES)]
-        return pltpu.make_async_copy(y4_ref.at[c, span], far, out_sem.at[t, c])
+        span = pl.ds(t * part, part)
+        far = flat_ref.at[span, pl.ds(c * LANES, LANES)]
+        return pltpu.make_async_copy(y_ref.at[c, span], far, out_sem.at[t, c])
 
     def step(t, carry):
         span = pl.ds(pl.multiple_of(t * part, 16), part)
@@ -318,10 +317,10 @@
         pltpu.with_memory_space_constraint(a, pltpu.HBM)
         for a in (turned, w_reduce, taps, w_expand, *params)
     ]
-    x4, z3, coef = pl.pallas_call(
+    x, z3, coef = pl.pallas_call(
         functools.partial(main_kernel, mesh_rows, mesh_cols, count, side, tiles),
         out_shape=(
-            jax.ShapeDtypeStruct((slabs, pixels, held, LANES), bf16),
+            jax.ShapeDtypeStruct((slabs, pixels * held, LANES), bf16),
             jax.ShapeDtypeStruct((pixels * held, channels), f32),
             jax.ShapeDtypeStruct((3, channels), f32),
         ),
@@ -354,12 +353,12 @@
         in_specs=[vmem] * 3,
         out_specs=anywhere,
         scratch_shapes=[
-            pltpu.VMEM((slabs, pixels, held, LANES), bf16),
+            pltpu.VMEM((slabs, pixels * held, LANES), bf16),
             pltpu.SemaphoreType.DMA((pieces, slabs)),
         ],
         compiler_params=pltpu.CompilerParams(vmem_limit_bytes=16 * 1024 * 1024),
         name="finish",
-    )(x4, z3, coef)
+    )(x, z3, coef)
     return out.reshape(side, side, held, channels).transpose(2, 0, 1, 3)
 
 

time: 48.4 us -> 46.5 us (0.961)
  Pallas kernels: 48.2 us -> 46.3 us
    pallas_call x1, Pallas kernels: 45 us -> 44 us  [local(): pl.pallas_call(functools.partial(main_kernel, mesh_rows, mesh_cols, count...]
    pallas_call x1, Pallas kernels: 3.22 us -> 2.29 us  [local(): pl.pallas_call(functools.partial(last_kernel, pieces), out_shape=jax.Shap...]
where the time goes in v1:
time: 46.5 us; the launch traced here: 46.4 us
  Pallas kernels  46.3 us (100%)
    pallas_call x1, Pallas kernels, local(): pl.pallas_call(functools.partial(main_kernel, mesh_rows, mesh_cols, count...  44 us
    pallas_call x1, Pallas kernels, local(): pl.pallas_call(functools.partial(last_kernel, pieces), out_shape=jax.Shap...  2.29 us

profile of v1, /device:TPU:0, one launch (start us, length us, event | category | flops | bytes accessed | tf_op | source)
XLA Modules:
  0.0 46.4 jit_solution(10465837165217388010)
XLA Ops:
  0.0 44.0 %bottlenecks.1 = (bf16[4,3136,128]{2,1,0:T(8,128)(2,1)S(1)}, f32[3136,512]{1,0:T(8,128)S(1)}, f32[3,512]{1,0:T(4,128)S(1)}) custom-call(bf16[784,4,512]{2,1,0:T(4,128)(2,1)} %bitcast.7, bf16[2,512,128]{2,1,0:T(8,128)(2,1)} %wr_hbm.1, bf16[2,1152,128]{2,1,0:T(8,128)(2,1)} %bitcast.8, bf16[2,128,512]{2,1,0:T(8,128)(2,1)} %we_hbm.1, f32[2,2,128]{2,1,0:T(2,128)} %gm_hbm.1, ...), custom_call_target="tpu_custom_call" | custom-call | tf_op jit(solution)/shard_map/bottlenecks/pallas_call | solution.py:320
  44.1 2.3 %finish.1 = bf16[784,4,512]{2,1,0:T(4,128)(2,1)} custom-call(bf16[4,3136,128]{2,1,0:T(8,128)(2,1)S(1)} %get-tuple-element.8.x_ref, f32[3136,512]{1,0:T(8,128)S(1)} %get-tuple-element.9.z3_ref, f32[3,512]{1,0:T(4,128)S(1)} %get-tuple-element.10.coef_ref), custom_call_target="tpu_custom_call" | custom-call | tf_op jit(solution)/shard_map/finish/pallas_call | solution.py:350

commit v2 on v1

v2 whole, which is shorter than its diff:
```python
import functools

import jax
import jax.numpy as jnp
from jax import lax
from jax.experimental import pallas as pl
from jax.experimental.pallas import tpu as pltpu
from jax.sharding import PartitionSpec as P

epsilon = 1e-05
ratio_max = 3.0
shift_max = 5.0
MESH = pl.DeviceIdType.MESH
LANES = 128
f32 = jnp.float32
bf16 = jnp.bfloat16


def coefficients(total, gain, bias, run_mean, run_var, count):
    mean_offset = total[0:1] / count
    center = run_mean + mean_offset
    variance = jnp.maximum(total[1:2] / count - mean_offset * mean_offset, 0.0)
    sigma = jnp.sqrt(variance + epsilon)
    run_sigma = jnp.sqrt(run_var + epsilon)
    ratio = jnp.clip(sigma / run_sigma, 1.0 / ratio_max, ratio_max)
    shift = jnp.clip(mean_offset / run_sigma, -shift_max, shift_max)
    scale = gain * (ratio / sigma)
    return scale, gain * shift + bias - center * scale


def flipped(index, bits):
    out, bit = index, 1
    while bit <= bits:
        if bits & bit:
            out = out + bit - 2 * bit * lax.rem(lax.div(index, bit), 2)
        bit *= 2
    return out


def tree_sum(parts):
    while len(parts) > 1:
        half = [a + b for a, b in zip(parts[0::2], parts[1::2])]
        parts = half + ([parts[-1]] if len(parts) % 2 else [])
    return parts[0]


def group_width(channels):
    return 2 * LANES if channels % (2 * LANES) == 0 else channels


def main_kernel(
    rows,
    cols,
    count,
    side,
    tiles,
    loads_in,
    img_ref,
    wr_hbm,
    ws_hbm,
    we_hbm,
    gm_hbm,
    bm_hbm,
    mm_hbm,
    vm_hbm,
    go_hbm,
    bo_hbm,
    mo_hbm,
    vo_hbm,
    x_ref,
    z3_ref,
    coef_ref,
    z_ref,
    h_ref,
    hc_ref,
    w2_ref,
    mid_buf,
    out_buf,
    wr_ref,
    we_ref,
    gm_ref,
    bm_ref,
    mm_ref,
    vm_ref,
    go_ref,
    bo_ref,
    mo_ref,
    vo_ref,
    in_sem,
    par_sem,
    tap_sem,
    send_sem,
    recv_sem,
):
    devices = rows * cols
    pixels, images, channels = img_ref.shape
    blocks, _, middle = wr_ref.shape
    slabs = channels // LANES
    width = group_width(channels)
    groups = channels // width
    per = width // LANES
    line = side * images
    tall = side // tiles
    part = tall * line
    total_rows = pixels * images
    my_row, my_col = lax.axis_index("row"), lax.axis_index("col")
    me = my_row * cols + my_col
    flat_ref = img_ref.reshape(total_rows, channels)
    zf_ref = z_ref.reshape(total_rows, middle)
    piece = total_rows // loads_in

    def slab_copy(t, c):
        span = pl.ds(t * piece, piece)
        far = flat_ref.at[span, pl.ds(c * LANES, LANES)]
        return pltpu.make_async_copy(far, x_ref.at[c, span], in_sem.at[t, c])

    pairs = (
        (wr_hbm, wr_ref), (mm_hbm, mm_ref), (we_hbm, we_ref), (gm_hbm, gm_ref),
        (bm_hbm, bm_ref), (vm_hbm, vm_ref), (go_hbm, go_ref), (bo_hbm, bo_ref),
        (mo_hbm, mo_ref), (vo_hbm, vo_ref),
    )
    loads = [pltpu.make_async_copy(a, b, par_sem.at[i]) for i, (a, b) in enumerate(pairs)]
    kernels = [
        pltpu.make_async_copy(
            ws_hbm.at[block],
            w2_ref.at[block, pl.ds(3 * i * middle, 9 * middle), pl.ds(i * middle, middle)],
            tap_sem.at[block, i],
        )
        for block in range(blocks)
        for i in range(2)
    ]
    for copy in loads[:2]:
        copy.start()
    for t in range(loads_in):
        for c in range(slabs):
            slab_copy(t, c).start()

    barrier = pltpu.get_barrier_semaphore()

    def to_all(act):
        if devices <= 64:
            if rows & (rows - 1) == 0 and cols & (cols - 1) == 0:
                far_rows = [flipped(my_row, i) for i in range(rows)]
                far_cols = [flipped(my_col, i) for i in range(cols)]
            else:
                far_rows = [lax.rem(my_row + i, rows) for i in range(rows)]
                far_cols = [lax.rem(my_col + i, cols) for i in range(cols)]
            for j in range(cols - 1, -1, -1):
                for i in range(rows - 1, -1, -1):
                    if i or j:
                        act((far_rows[i], far_cols[j]))
        else:

            def step(i, c):
                other = lax.rem(me + i, devices)
                act((lax.div(other, cols), lax.rem(other, cols)))
                return c

            lax.fori_loop(1, devices, step, 0)

    to_all(
        lambda there: pl.semaphore_signal(
            barrier, inc=1, device_id=there, device_id_type=MESH
        )
    )

    def slots(ref, index):
        others = ref.at[pl.ds(0, devices - 1)]
        return pltpu.make_async_remote_copy(
            src_ref=others,
            dst_ref=others,
            send_sem=send_sem.at[index],
            recv_sem=recv_sem.at[index],
            device_id=(lax.rem(my_row + 1, rows), my_col),
            device_id_type=MESH,
        )

    def share(ref, sums, index):
        for i in range(2):
            ref[me, pl.ds(i, 1), :] = jnp.sum(sums[i], axis=0, keepdims=True)
        if index == 0:
            pl.semaphore_wait(barrier, devices - 1)

        def send(there):
            pltpu.make_async_remote_copy(
                src_ref=ref.at[me],
                dst_ref=ref.at[me],
                send_sem=send_sem.at[index],
                recv_sem=recv_sem.at[index],
                device_id=there,
                device_id_type=MESH,
            ).start()

        to_all(send)

    def collect(ref, index):
        slots(ref, index).wait_recv()
        if devices <= 64:
            return tree_sum([ref[d] for d in range(devices)])
        return jnp.sum(ref[...], axis=0)

    def moments(z, mean, sums):
        d = (z - mean).reshape(-1, 16, z.shape[-1])
        return sums[0] + jnp.sum(d, axis=0), sums[1] + jnp.sum(d * d, axis=0)

    def zeros(c):
        return (jnp.zeros((16, c), f32), jnp.zeros((16, c), f32))

    hc_ref[0] = jnp.zeros((line, 3 * middle), bf16)
    hc_ref[side + 1] = jnp.zeros((line, 3 * middle), bf16)
    empty = jnp.zeros((3 * middle, middle), bf16)
    for block in range(blocks):
        w2_ref[block, pl.ds(9 * middle, 3 * middle), 0:middle] = empty
        w2_ref[block, pl.ds(0, 3 * middle), middle : 2 * middle] = empty
    for copy in loads[:2]:
        copy.wait()
    place = lax.broadcasted_iota(jnp.int32, (1, line, 1), 1)

    def updated(start, size, g, coef):
        scale, offset = coef
        new = []
        for c in range(per):
            lanes = slice(c * LANES, (c + 1) * LANES)
            slab = g * per + c
            span = pl.ds(start, size)
            z = z3_ref[slab, span, :] * scale[:, lanes] + offset[:, lanes]
            y = jnp.maximum(z + x_ref[slab, span, :].astype(f32), 0.0).astype(bf16)
            x_ref[slab, span, :] = y
            new.append(y)
        return new

    def halves(start, size):
        first = (size // 2 + 15) // 16 * 16
        return ((start, first), (start + first, size - first))

    per_block = 2 + groups

    def index_of(block, stage):
        return per_block * block + stage

    mids = lambda block, i: mid_buf.at[2 * block + i]
    outs = lambda block, g: out_buf.at[block, g]

    sums = zeros(middle)
    mean_one = mm_ref[0, pl.ds(0, 1), :]
    for t in range(loads_in):
        for c in range(slabs):
            slab_copy(t, c).wait()
        for start, size in halves(t * piece, piece):
            x = jnp.concatenate([x_ref[c, pl.ds(start, size), :] for c in range(slabs)], axis=1)
            z = jnp.dot(x, wr_ref[0], preferred_element_type=f32)
            zf_ref[pl.ds(start, size), :] = z
            sums = moments(z, mean_one, sums)
    share(mids(0, 0), sums, index_of(0, 0))
    for copy in loads[2:] + kernels:
        copy.start()
    for copy in loads[2:] + kernels:
        copy.wait()

    for block in range(blocks):
        mean_one = mm_ref[block, pl.ds(0, 1), :]
        mean_two = mm_ref[block, pl.ds(1, 1), :]
        scale1, offset1 = coefficients(
            collect(mids(block, 0), index_of(block, 0)),
            gm_ref[block, pl.ds(0, 1), :], bm_ref[block, pl.ds(0, 1), :],
            mean_one, vm_ref[block, pl.ds(0, 1), :], count,
        )

        for t in range(tiles):
            z = zf_ref[pl.ds(t * part, part), :]
            h = jnp.maximum(z * scale1 + offset1, 0.0)
            left = pltpu.roll(h, images, 0).reshape(tall, line, middle)
            right = pltpu.roll(h, part - images, 0).reshape(tall, line, middle)
            left = jnp.where(place >= images, left, 0.0)
            right = jnp.where(place < line - images, right, 0.0)
            taps = (left, h.reshape(tall, line, middle), right)
            for i, tap in enumerate(taps):
                lanes = slice(i * middle, (i + 1) * middle)
                hc_ref[pl.ds(t * tall + 1, tall), :, lanes] = tap.astype(bf16)

        sums = zeros(middle)
        for t in range(tiles):
            v = hc_ref[pl.ds(t * tall, tall + 2)].reshape(tall // 2 + 1, 2, line, 3 * middle)
            lhs = jnp.concatenate(
                [v[:-1, 0], v[:-1, 1], v[1:, 0], v[1:, 1]], axis=-1
            ).reshape(part // 2, 12 * middle)
            z = jnp.dot(lhs, w2_ref[block], preferred_element_type=f32)
            for i in range(2):
                half = z[:, i * middle : (i + 1) * middle]
                z_ref[pl.ds(t * (tall // 2), tall // 2), i] = half.reshape(
                    tall // 2, line, middle
                )
                sums = moments(half, mean_two, sums)
        share(mids(block, 1), sums, index_of(block, 1))
        scale2, offset2 = coefficients(
            collect(mids(block, 1), index_of(block, 1)),
            gm_ref[block, pl.ds(1, 1), :], bm_ref[block, pl.ds(1, 1), :],
            mean_two, vm_ref[block, pl.ds(1, 1), :], count,
        )

        for g in range(groups):
            wide = slice(g * width, (g + 1) * width)
            mean_out = mo_ref[pl.ds(block, 1), wide]
            sums = zeros(width)
            for t in range(tiles):
                span = pl.ds(t * part, part)
                if g == 0:
                    z = zf_ref[span, :]
                    h = jnp.maximum(z * scale2 + offset2, 0.0).astype(bf16)
                    h_ref[span, :] = h
                else:
                    h = h_ref[span, :]
                z = jnp.dot(h, we_ref[block, :, wide], preferred_element_type=f32)
                for c in range(per):
                    z3_ref[g * per + c, span, :] = z[:, c * LANES : (c + 1) * LANES]
                sums = moments(z, mean_out, sums)
            share(outs(block, g), sums, index_of(block, 2 + g))

        last = block == blocks - 1
        if not last:
            mean_one = mm_ref[block + 1, pl.ds(0, 1), :]
            sums = zeros(middle)
        for g in range(groups):
            wide = slice(g * width, (g + 1) * width)
            coef = coefficients(
                collect(outs(block, g), index_of(block, 2 + g)),
                go_ref[pl.ds(block, 1), wide], bo_ref[pl.ds(block, 1), wide],
                mo_ref[pl.ds(block, 1), wide], vo_ref[pl.ds(block, 1), wide], count,
            )
            if last and g == groups - 1:
                for i in range(2):
                    coef_ref[pl.ds(i, 1), :] = coef[i]
                break
            for t in range(tiles):
                y = updated(t * part, part, g, coef)
                if last:
                    continue
                span = pl.ds(t * part, part)
                y = jnp.concatenate(y, axis=1)
                z = jnp.dot(y, wr_ref[block + 1, wide, :], preferred_element_type=f32)
                if g:
                    z = z + zf_ref[span, :]
                zf_ref[span, :] = z
                if g == groups - 1:
                    sums = moments(z, mean_one, sums)
        if not last:
            share(mids(block + 1, 0), sums, index_of(block + 1, 0))

    for block in range(blocks):
        for i in range(2):
            slots(mids(block, i), index_of(block, i)).wait_send()
        for g in range(groups):
            slots(outs(block, g), index_of(block, 2 + g)).wait_send()


def last_kernel(pieces, x_ref, z3_ref, coef_ref, o_ref, y_ref, out_sem, old_sem):
    slabs = x_ref.shape[0]
    pixels, images, channels = o_ref.shape
    part = pixels // pieces * images
    per = coef_ref.shape[1] // LANES
    done = slabs - per
    flat_ref = o_ref.reshape(pixels * images, channels)

    def old_copy(c):
        return pltpu.make_async_copy(
            x_ref.at[c], flat_ref.at[:, pl.ds(c * LANES, LANES)], old_sem.at[c]
        )

    def slab_copy(t, c):
        span = pl.ds(t * part, part)
        far = flat_ref.at[span, pl.ds((done + c) * LANES, LANES)]
        return pltpu.make_async_copy(y_ref.at[c, span], far, out_sem.at[t, c])

    for c in range(done):
        old_copy(c).start()

    def step(t, carry):
        span = pl.ds(pl.multiple_of(t * part, 16), part)
        for c in range(per):
            lanes = slice(c * LANES, (c + 1) * LANES)
            scale, offset = (coef_ref[pl.ds(i, 1), lanes] for i in range(2))
            z = z3_ref[done + c, span, :] * scale + offset
            y = jnp.maximum(z + x_ref[done + c, span, :].astype(f32), 0.0)
            y_ref[c, span, :] = y.astype(bf16)
            slab_copy(t, c).start()
        return carry

    lax.fori_loop(0, pieces, step, 0)
    for c in range(done):
        old_copy(c).wait()
    for t in range(pieces):
        for c in range(per):
            slab_copy(t, c).wait()


def local(mesh_rows, mesh_cols, images, w_reduce, w_spatial, w_expand, *params):
    held, side, _, channels = images.shape
    blocks, _, middle = w_reduce.shape
    devices = mesh_rows * mesh_cols
    count = float(held * side * side * devices)
    tiles = next(t for t in (TILES, 2, 1) if side % (2 * t) == 0)
    slabs = channels // LANES
    pixels = side * side
    loads_in = next(t for t in (4, 2, 1) if pixels * held % (16 * t) == 0)
    width = group_width(channels)
    groups = channels // width
    vmem = pl.BlockSpec(memory_space=pltpu.VMEM)
    anywhere = pl.BlockSpec(memory_space=pltpu.HBM)
    turned = images.transpose(1, 2, 0, 3).reshape(pixels, held, channels)
    taps = w_spatial.reshape(blocks, 9 * middle, middle)
    operands = [
        pltpu.with_memory_space_constraint(a, pltpu.HBM)
        for a in (turned, w_reduce, taps, w_expand, *params)
    ]
    x, z3, coef = pl.pallas_call(
        functools.partial(main_kernel, mesh_rows, mesh_cols, count, side, tiles, loads_in),
        out_shape=(
            jax.ShapeDtypeStruct((slabs, pixels * held, LANES), bf16),
            jax.ShapeDtypeStruct((slabs, pixels * held, LANES), f32),
            jax.ShapeDtypeStruct((2, width), f32),
        ),
        in_specs=[anywhere] * 12,
        out_specs=(vmem, vmem, vmem),
        scratch_shapes=[
            pltpu.VMEM((side // 2, 2, side * held, middle), f32),
            pltpu.VMEM((pixels * held, middle), bf16),
            pltpu.VMEM((side + 2, side * held, 3 * middle), bf16),
            pltpu.VMEM((blocks, 12 * middle, 2 * middle), bf16),
            pltpu.VMEM((2 * blocks, devices, 2, middle), f32),
            pltpu.VMEM((blocks, groups, devices, 2, width), f32),
            pltpu.VMEM(w_reduce.shape, bf16),
            pltpu.VMEM(w_expand.shape, bf16),
            *(pltpu.VMEM(p.shape, f32) for p in params),
            pltpu.SemaphoreType.DMA((loads_in, slabs)),
            pltpu.SemaphoreType.DMA((10,)),
            pltpu.SemaphoreType.DMA((blocks, 2)),
            pltpu.SemaphoreType.DMA(((2 + groups) * blocks,)),
            pltpu.SemaphoreType.DMA(((2 + groups) * blocks,)),
        ],
        compiler_params=pltpu.CompilerParams(
            collective_id=0, has_side_effects=True, vmem_limit_bytes=LIMIT * 1024 * 1024
        ),
        name="bottlenecks",
    )(*operands)
    pieces = side // 4 if side % 4 == 0 else 1
    out = pl.pallas_call(
        functools.partial(last_kernel, pieces),
        out_shape=jax.ShapeDtypeStruct((pixels, held, channels), bf16),
        in_specs=[vmem] * 3,
        out_specs=anywhere,
        scratch_shapes=[
            pltpu.VMEM((width // LANES, pixels * held, LANES), bf16),
            pltpu.SemaphoreType.DMA((pieces, width // LANES)),
            pltpu.SemaphoreType.DMA((slabs,)),
        ],
        compiler_params=pltpu.CompilerParams(vmem_limit_bytes=16 * 1024 * 1024),
        name="finish",
    )(x, z3, coef)
    return out.reshape(side, side, held, channels).transpose(2, 0, 1, 3)


TILES = 2
LIMIT = 32


def solution(mesh):
    spec = P(("row", "col"), None, None, None)
    return jax.shard_map(
        functools.partial(local, mesh.shape["row"], mesh.shape["col"]),
        mesh=mesh,
        in_specs=(spec,) + (P(),) * 11,
        out_specs=spec,
        check_vma=False,
    )
```

time: 46.5 us -> 44 us (0.946)
  Pallas kernels: 46.3 us -> 43.9 us
    pallas_call x1, Pallas kernels: 44 us -> 42 us  [local(): pl.pallas_call(functools.partial(main_kernel, mesh_rows, mesh_cols, count...]
    pallas_call x1, Pallas kernels: 2.29 us -> 1.82 us  [local(): pl.pallas_call(functools.partial(last_kernel, pieces), out_shape=jax.Shap...]
where the time goes in v2:
time: 44 us; the launch traced here: 43.9 us
  Pallas kernels  43.9 us (100%)
    pallas_call x1, Pallas kernels, local(): pl.pallas_call(functools.partial(main_kernel, mesh_rows, mesh_cols, count...  42 us
    pallas_call x1, Pallas kernels, local(): pl.pallas_call(functools.partial(last_kernel, pieces), out_shape=jax.Shap...  1.82 us

profile of v2, /device:TPU:0, one launch (start us, length us, event | category | flops | bytes accessed | tf_op | source)
XLA Modules:
  0.0 43.9 jit_solution(2187281138164399952)
XLA Ops:
  0.0 42.0 %bottlenecks.1 = (bf16[4,3136,128]{2,1,0:T(8,128)(2,1)S(1)}, f32[4,3136,128]{2,1,0:T(8,128)S(1)}, f32[2,256]{1,0:T(2,128)S(1)}) custom-call(bf16[784,4,512]{2,1,0:T(4,128)(2,1)} %bitcast.7, bf16[2,512,128]{2,1,0:T(8,128)(2,1)} %wr_hbm.1, bf16[2,1152,128]{2,1,0:T(8,128)(2,1)} %bitcast.8, bf16[2,128,512]{2,1,0:T(8,128)(2,1)} %we_hbm.1, f32[2,2,128]{2,1,0:T(2,128)} %gm_hbm.1, ...), custom_call_target="tpu_custom_call" | custom-call | tf_op jit(solution)/shard_map/bottlenecks/pallas_call | solution.py:415
  42.0 1.8 %finish.1 = bf16[784,4,512]{2,1,0:T(4,128)(2,1)} custom-call(bf16[4,3136,128]{2,1,0:T(8,128)(2,1)S(1)} %get-tuple-element.8.x_ref, f32[4,3136,128]{2,1,0:T(8,128)S(1)} %get-tuple-element.9.z3_ref, f32[2,256]{1,0:T(2,128)S(1)} %get-tuple-element.10.coef_ref), custom_call_target="tpu_custom_call" | custom-call | tf_op jit(solution)/shard_map/finish/pallas_call | solution.py:446

commit v3 on v2

--- a/solution.py
+++ b/solution.py
@@ -16,16 +16,15 @@
 bf16 = jnp.bfloat16
 
 
-def coefficients(total, gain, bias, run_mean, run_var, count):
+def coefficients(total, gain, bias, run_var, count):
     mean_offset = total[0:1] / count
-    center = run_mean + mean_offset
     variance = jnp.maximum(total[1:2] / count - mean_offset * mean_offset, 0.0)
     sigma = jnp.sqrt(variance + epsilon)
     run_sigma = jnp.sqrt(run_var + epsilon)
     ratio = jnp.clip(sigma / run_sigma, 1.0 / ratio_max, ratio_max)
     shift = jnp.clip(mean_offset / run_sigma, -shift_max, shift_max)
     scale = gain * (ratio / sigma)
-    return scale, gain * shift + bias - center * scale
+    return scale, gain * shift + bias - mean_offset * scale
 
 
 def flipped(index, bits):
@@ -115,11 +114,14 @@
         return pltpu.make_async_copy(far, x_ref.at[c, span], in_sem.at[t, c])
 
     pairs = (
-        (wr_hbm, wr_ref), (mm_hbm, mm_ref), (we_hbm, we_ref), (gm_hbm, gm_ref),
+        (wr_hbm.at[0], wr_ref.at[0]), (mm_hbm, mm_ref), (we_hbm, we_ref.at[:, pl.ds(0, middle)]), (gm_hbm, gm_ref),
         (bm_hbm, bm_ref), (vm_hbm, vm_ref), (go_hbm, go_ref), (bo_hbm, bo_ref),
         (mo_hbm, mo_ref), (vo_hbm, vo_ref),
     )
     loads = [pltpu.make_async_copy(a, b, par_sem.at[i]) for i, (a, b) in enumerate(pairs)]
+    if blocks > 1:
+        rest = pl.ds(1, blocks - 1)
+        loads.append(pltpu.make_async_copy(wr_hbm.at[rest], wr_ref.at[rest], par_sem.at[len(pairs)]))
     kernels = [
         pltpu.make_async_copy(
             ws_hbm.at[block],
@@ -129,12 +131,6 @@
         for block in range(blocks)
         for i in range(2)
     ]
-    for copy in loads[:2]:
-        copy.start()
-    for t in range(loads_in):
-        for c in range(slabs):
-            slab_copy(t, c).start()
-
     barrier = pltpu.get_barrier_semaphore()
 
     def to_all(act):
@@ -158,11 +154,17 @@
 
             lax.fori_loop(1, devices, step, 0)
 
+    for copy in loads[:2]:
+        copy.start()
     to_all(
         lambda there: pl.semaphore_signal(
             barrier, inc=1, device_id=there, device_id_type=MESH
         )
     )
+
+    for t in range(loads_in):
+        for c in range(slabs):
+            slab_copy(t, c).start()
 
     def slots(ref, index):
         others = ref.at[pl.ds(0, devices - 1)]
@@ -199,19 +201,13 @@
             return tree_sum([ref[d] for d in range(devices)])
         return jnp.sum(ref[...], axis=0)
 
-    def moments(z, mean, sums):
-        d = (z - mean).reshape(-1, 16, z.shape[-1])
+    def moments(d, sums):
+        d = d.reshape(-1, 16, d.shape[-1])
         return sums[0] + jnp.sum(d, axis=0), sums[1] + jnp.sum(d * d, axis=0)
 
     def zeros(c):
         return (jnp.zeros((16, c), f32), jnp.zeros((16, c), f32))
 
-    hc_ref[0] = jnp.zeros((line, 3 * middle), bf16)
-    hc_ref[side + 1] = jnp.zeros((line, 3 * middle), bf16)
-    empty = jnp.zeros((3 * middle, middle), bf16)
-    for block in range(blocks):
-        w2_ref[block, pl.ds(9 * middle, 3 * middle), 0:middle] = empty
-        w2_ref[block, pl.ds(0, 3 * middle), middle : 2 * middle] = empty
     for copy in loads[:2]:
         copy.wait()
     place = lax.broadcasted_iota(jnp.int32, (1, line, 1), 1)
@@ -224,7 +220,7 @@
             slab = g * per + c
             span = pl.ds(start, size)
             z = z3_ref[slab, span, :] * scale[:, lanes] + offset[:, lanes]
-            y = jnp.maximum(z + x_ref[slab, span, :].astype(f32), 0.0).astype(bf16)
+            y = jnp.maximum(z.astype(bf16) + x_ref[slab, span, :], 0)
             x_ref[slab, span, :] = y
             new.append(y)
         return new
@@ -248,22 +244,39 @@
             slab_copy(t, c).wait()
         for start, size in halves(t * piece, piece):
             x = jnp.concatenate([x_ref[c, pl.ds(start, size), :] for c in range(slabs)], axis=1)
-            z = jnp.dot(x, wr_ref[0], preferred_element_type=f32)
+            z = jnp.dot(x, wr_ref[0], preferred_element_type=f32) - mean_one
             zf_ref[pl.ds(start, size), :] = z
-            sums = moments(z, mean_one, sums)
+            sums = moments(z, sums)
     share(mids(0, 0), sums, index_of(0, 0))
     for copy in loads[2:] + kernels:
         copy.start()
+    hc_ref[0] = jnp.zeros((line, 3 * middle), bf16)
+    hc_ref[side + 1] = jnp.zeros((line, 3 * middle), bf16)
+    empty = jnp.zeros((3 * middle, middle), bf16)
+    for block in range(blocks):
+        w2_ref[block, pl.ds(9 * middle, 3 * middle), 0:middle] = empty
+        w2_ref[block, pl.ds(0, 3 * middle), middle : 2 * middle] = empty
     for copy in loads[2:] + kernels:
         copy.wait()
-
     for block in range(blocks):
-        mean_one = mm_ref[block, pl.ds(0, 1), :]
+        left_over = -mo_ref[pl.ds(block, 1), :]
+        digits = []
+        for _ in range(3):
+            digits.append(left_over.astype(bf16).astype(f32))
+            left_over = left_over - digits[-1]
+        place_in = lax.broadcasted_iota(jnp.int32, (middle, channels), 0)
+        below = jnp.zeros((middle, channels), f32)
+        for i, digit in enumerate(digits):
+            below = jnp.where(place_in == i, digit, below)
+        we_ref[block, pl.ds(middle, middle), :] = below.astype(bf16)
+    ones = (lax.broadcasted_iota(jnp.int32, (part, LANES), 1) < 3).astype(f32).astype(bf16)
+
+    for block in range(blocks):
         mean_two = mm_ref[block, pl.ds(1, 1), :]
         scale1, offset1 = coefficients(
             collect(mids(block, 0), index_of(block, 0)),
             gm_ref[block, pl.ds(0, 1), :], bm_ref[block, pl.ds(0, 1), :],
-            mean_one, vm_ref[block, pl.ds(0, 1), :], count,
+            vm_ref[block, pl.ds(0, 1), :], count,
         )
 
         for t in range(tiles):
@@ -286,34 +299,34 @@
             ).reshape(part // 2, 12 * middle)
             z = jnp.dot(lhs, w2_ref[block], preferred_element_type=f32)
             for i in range(2):
-                half = z[:, i * middle : (i + 1) * middle]
+                half = z[:, i * middle : (i + 1) * middle] - mean_two
                 z_ref[pl.ds(t * (tall // 2), tall // 2), i] = half.reshape(
                     tall // 2, line, middle
                 )
-                sums = moments(half, mean_two, sums)
+                sums = moments(half, sums)
         share(mids(block, 1), sums, index_of(block, 1))
         scale2, offset2 = coefficients(
             collect(mids(block, 1), index_of(block, 1)),
             gm_ref[block, pl.ds(1, 1), :], bm_ref[block, pl.ds(1, 1), :],
-            mean_two, vm_ref[block, pl.ds(1, 1), :], count,
+            vm_ref[block, pl.ds(1, 1), :], count,
         )
 
         for g in range(groups):
             wide = slice(g * width, (g + 1) * width)
-            mean_out = mo_ref[pl.ds(block, 1), wide]
             sums = zeros(width)
             for t in range(tiles):
                 span = pl.ds(t * part, part)
                 if g == 0:
                     z = zf_ref[span, :]
-                    h = jnp.maximum(z * scale2 + offset2, 0.0).astype(bf16)
+                    h = jnp.maximum((z * scale2 + offset2).astype(bf16), 0)
                     h_ref[span, :] = h
                 else:
                     h = h_ref[span, :]
-                z = jnp.dot(h, we_ref[block, :, wide], preferred_element_type=f32)
+                lhs = jnp.concatenate([h, ones], axis=1)
+                z = jnp.dot(lhs, we_ref[block, :, wide], preferred_element_type=f32)
                 for c in range(per):
                     z3_ref[g * per + c, span, :] = z[:, c * LANES : (c + 1) * LANES]
-                sums = moments(z, mean_out, sums)
+                sums = moments(z, sums)
             share(outs(block, g), sums, index_of(block, 2 + g))
 
         last = block == blocks - 1
@@ -325,7 +338,7 @@
             coef = coefficients(
                 collect(outs(block, g), index_of(block, 2 + g)),
                 go_ref[pl.ds(block, 1), wide], bo_ref[pl.ds(block, 1), wide],
-                mo_ref[pl.ds(block, 1), wide], vo_ref[pl.ds(block, 1), wide], count,
+                vo_ref[pl.ds(block, 1), wide], count,
             )
             if last and g == groups - 1:
                 for i in range(2):
@@ -338,11 +351,10 @@
                 span = pl.ds(t * part, part)
                 y = jnp.concatenate(y, axis=1)
                 z = jnp.dot(y, wr_ref[block + 1, wide, :], preferred_element_type=f32)
-                if g:
-                    z = z + zf_ref[span, :]
+                z = z + zf_ref[span, :] if g else z - mean_one
                 zf_ref[span, :] = z
                 if g == groups - 1:
-                    sums = moments(z, mean_one, sums)
+                    sums = moments(z, sums)
         if not last:
             share(mids(block + 1, 0), sums, index_of(block + 1, 0))
 
@@ -380,8 +392,8 @@
             lanes = slice(c * LANES, (c + 1) * LANES)
             scale, offset = (coef_ref[pl.ds(i, 1), lanes] for i in range(2))
             z = z3_ref[done + c, span, :] * scale + offset
-            y = jnp.maximum(z + x_ref[done + c, span, :].astype(f32), 0.0)
-            y_ref[c, span, :] = y.astype(bf16)
+            y = z.astype(bf16) + x_ref[done + c, span, :]
+            y_ref[c, span, :] = jnp.maximum(y, 0)
             slab_copy(t, c).start()
         return carry
 
@@ -429,10 +441,10 @@
             pltpu.VMEM((2 * blocks, devices, 2, middle), f32),
             pltpu.VMEM((blocks, groups, devices, 2, width), f32),
             pltpu.VMEM(w_reduce.shape, bf16),
-            pltpu.VMEM(w_expand.shape, bf16),
+            pltpu.VMEM((blocks, 2 * middle, channels), bf16),
             *(pltpu.VMEM(p.shape, f32) for p in params),
             pltpu.SemaphoreType.DMA((loads_in, slabs)),
-            pltpu.SemaphoreType.DMA((10,)),
+            pltpu.SemaphoreType.DMA((11,)),
             pltpu.SemaphoreType.DMA((blocks, 2)),
             pltpu.SemaphoreType.DMA(((2 + groups) * blocks,)),
             pltpu.SemaphoreType.DMA(((2 + groups) * blocks,)),

time: 44 us -> 43.9 us (level)
  no operation moved by 1% of the time
where the time goes in v3:
time: 43.9 us; the launch traced here: 43.7 us
  Pallas kernels  43.7 us (100%)
    pallas_call x1, Pallas kernels, local(): pl.pallas_call(functools.partial(main_kernel, mesh_rows, mesh_cols, count...  41.9 us
    pallas_call x1, Pallas kernels, local(): pl.pallas_call(functools.partial(last_kernel, pieces), out_shape=jax.Shap...  1.82 us

profile of v3, /device:TPU:0, one launch (start us, length us, event | category | flops | bytes accessed | tf_op | source)
XLA Modules:
  0.0 43.7 jit_solution(6531246879805496509)
XLA Ops:
  0.0 41.9 %bottlenecks.1 = (bf16[4,3136,128]{2,1,0:T(8,128)(2,1)S(1)}, f32[4,3136,128]{2,1,0:T(8,128)S(1)}, f32[2,256]{1,0:T(2,128)S(1)}) custom-call(bf16[784,4,512]{2,1,0:T(4,128)(2,1)} %bitcast.7, bf16[2,512,128]{2,1,0:T(8,128)(2,1)} %wr_hbm.1, bf16[2,1152,128]{2,1,0:T(8,128)(2,1)} %bitcast.8, bf16[2,128,512]{2,1,0:T(8,128)(2,1)} %we_hbm.1, f32[2,2,128]{2,1,0:T(2,128)} %gm_hbm.1, ...), custom_call_target="tpu_custom_call" | custom-call | tf_op jit(solution)/shard_map/bottlenecks/pallas_call | solution.py:427
  41.9 1.8 %finish.1 = bf16[784,4,512]{2,1,0:T(4,128)(2,1)} custom-call(bf16[4,3136,128]{2,1,0:T(8,128)(2,1)S(1)} %get-tuple-element.8.x_ref, f32[4,3136,128]{2,1,0:T(8,128)S(1)} %get-tuple-element.9.z3_ref, f32[2,256]{1,0:T(2,128)S(1)} %get-tuple-element.10.coef_ref), custom_call_target="tpu_custom_call" | custom-call | tf_op jit(solution)/shard_map/finish/pallas_call | solution.py:458

commit v4 on v3

--- a/solution.py
+++ b/solution.py
@@ -70,7 +70,6 @@
     z3_ref,
     coef_ref,
     z_ref,
-    h_ref,
     hc_ref,
     w2_ref,
     mid_buf,
@@ -107,11 +106,12 @@
     flat_ref = img_ref.reshape(total_rows, channels)
     zf_ref = z_ref.reshape(total_rows, middle)
     piece = total_rows // loads_in
+    chunk = next(16 * k for k in (14, 7, 4, 2, 1) if total_rows % (16 * k) == 0)
 
     def slab_copy(t, c):
         span = pl.ds(t * piece, piece)
         far = flat_ref.at[span, pl.ds(c * LANES, LANES)]
-        return pltpu.make_async_copy(far, x_ref.at[c, span], in_sem.at[t, c])
+        return pltpu.make_async_copy(far, x_ref.at[c, span], in_sem.at[t])
 
     pairs = (
         (wr_hbm.at[0], wr_ref.at[0]), (mm_hbm, mm_ref), (we_hbm, we_ref.at[:, pl.ds(0, middle)]), (gm_hbm, gm_ref),
@@ -196,7 +196,9 @@
         to_all(send)
 
     def collect(ref, index):
-        slots(ref, index).wait_recv()
+        exchange = slots(ref, index)
+        exchange.wait_send()
+        exchange.wait_recv()
         if devices <= 64:
             return tree_sum([ref[d] for d in range(devices)])
         return jnp.sum(ref[...], axis=0)
@@ -212,7 +214,7 @@
         copy.wait()
     place = lax.broadcasted_iota(jnp.int32, (1, line, 1), 1)
 
-    def updated(start, size, g, coef):
+    def updated(start, size, g, coef, keep):
         scale, offset = coef
         new = []
         for c in range(per):
@@ -221,7 +223,8 @@
             span = pl.ds(start, size)
             z = z3_ref[slab, span, :] * scale[:, lanes] + offset[:, lanes]
             y = jnp.maximum(z.astype(bf16) + x_ref[slab, span, :], 0)
-            x_ref[slab, span, :] = y
+            if keep:
+                x_ref[slab, span, :] = y
             new.append(y)
         return new
 
@@ -240,8 +243,8 @@
     sums = zeros(middle)
     mean_one = mm_ref[0, pl.ds(0, 1), :]
     for t in range(loads_in):
-        for c in range(slabs):
-            slab_copy(t, c).wait()
+        tile = x_ref.at[:, pl.ds(t * piece, piece)]
+        pltpu.make_async_copy(tile, tile, in_sem.at[t]).wait()
         for start, size in halves(t * piece, piece):
             x = jnp.concatenate([x_ref[c, pl.ds(start, size), :] for c in range(slabs)], axis=1)
             z = jnp.dot(x, wr_ref[0], preferred_element_type=f32) - mean_one
@@ -316,12 +319,11 @@
             sums = zeros(width)
             for t in range(tiles):
                 span = pl.ds(t * part, part)
+                h = zf_ref[span, :]
                 if g == 0:
-                    z = zf_ref[span, :]
-                    h = jnp.maximum((z * scale2 + offset2).astype(bf16), 0)
-                    h_ref[span, :] = h
-                else:
-                    h = h_ref[span, :]
+                    h = jnp.maximum(h * scale2 + offset2, 0.0)
+                    zf_ref[span, :] = h
+                h = h.astype(bf16)
                 lhs = jnp.concatenate([h, ones], axis=1)
                 z = jnp.dot(lhs, we_ref[block, :, wide], preferred_element_type=f32)
                 for c in range(per):
@@ -333,6 +335,7 @@
         if not last:
             mean_one = mm_ref[block + 1, pl.ds(0, 1), :]
             sums = zeros(middle)
+        coefs = []
         for g in range(groups):
             wide = slice(g * width, (g + 1) * width)
             coef = coefficients(
@@ -340,12 +343,13 @@
                 go_ref[pl.ds(block, 1), wide], bo_ref[pl.ds(block, 1), wide],
                 vo_ref[pl.ds(block, 1), wide], count,
             )
+            coefs.append(coef)
             if last and g == groups - 1:
                 for i in range(2):
                     coef_ref[pl.ds(i, 1), :] = coef[i]
                 break
             for t in range(tiles):
-                y = updated(t * part, part, g, coef)
+                y = updated(t * part, part, g, coef, last)
                 if last:
                     continue
                 span = pl.ds(t * part, part)
@@ -358,11 +362,12 @@
         if not last:
             share(mids(block + 1, 0), sums, index_of(block + 1, 0))
 
-    for block in range(blocks):
-        for i in range(2):
-            slots(mids(block, i), index_of(block, i)).wait_send()
-        for g in range(groups):
-            slots(outs(block, g), index_of(block, 2 + g)).wait_send()
+            def keep(t, carry):
+                for g in range(groups):
+                    updated(pl.multiple_of(t * chunk, 16), chunk, g, coefs[g], True)
+                return carry
+
+            lax.fori_loop(0, total_rows // chunk, keep, 0)
 
 
 def last_kernel(pieces, x_ref, z3_ref, coef_ref, o_ref, y_ref, out_sem, old_sem):
@@ -435,7 +440,6 @@
         out_specs=(vmem, vmem, vmem),
         scratch_shapes=[
             pltpu.VMEM((side // 2, 2, side * held, middle), f32),
-            pltpu.VMEM((pixels * held, middle), bf16),
             pltpu.VMEM((side + 2, side * held, 3 * middle), bf16),
             pltpu.VMEM((blocks, 12 * middle, 2 * middle), bf16),
             pltpu.VMEM((2 * blocks, devices, 2, middle), f32),
@@ -443,7 +447,7 @@
             pltpu.VMEM(w_reduce.shape, bf16),
             pltpu.VMEM((blocks, 2 * middle, channels), bf16),
             *(pltpu.VMEM(p.shape, f32) for p in params),
-            pltpu.SemaphoreType.DMA((loads_in, slabs)),
+            pltpu.SemaphoreType.DMA((loads_in,)),
             pltpu.SemaphoreType.DMA((11,)),
             pltpu.SemaphoreType.DMA((blocks, 2)),
             pltpu.SemaphoreType.DMA(((2 + groups) * blocks,)),

time: 43.9 us -> 43.5 us (level)
  no operation moved by 1% of the time
where the time goes in v4:
time: 43.5 us; the launch traced here: 43.4 us
  Pallas kernels  43.3 us (100%)
    pallas_call x1, Pallas kernels, local(): pl.pallas_call(functools.partial(main_kernel, mesh_rows, mesh_cols, count...  41.5 us
    pallas_call x1, Pallas kernels, local(): pl.pallas_call(functools.partial(last_kernel, pieces), out_shape=jax.Shap...  1.82 us

profile of v4, /device:TPU:0, one launch (start us, length us, event | category | flops | bytes accessed | tf_op | source)
XLA Modules:
  0.0 43.4 jit_solution(13112106831274995360)
XLA Ops:
  0.0 41.5 %bottlenecks.1 = (bf16[4,3136,128]{2,1,0:T(8,128)(2,1)S(1)}, f32[4,3136,128]{2,1,0:T(8,128)S(1)}, f32[2,256]{1,0:T(2,128)S(1)}) custom-call(bf16[784,4,512]{2,1,0:T(4,128)(2,1)} %bitcast.7, bf16[2,512,128]{2,1,0:T(8,128)(2,1)} %wr_hbm.1, bf16[2,1152,128]{2,1,0:T(8,128)(2,1)} %bitcast.8, bf16[2,128,512]{2,1,0:T(8,128)(2,1)} %we_hbm.1, f32[2,2,128]{2,1,0:T(2,128)} %gm_hbm.1, ...), custom_call_target="tpu_custom_call" | custom-call | tf_op jit(solution)/shard_map/bottlenecks/pallas_call | solution.py:432
  41.5 1.8 %finish.1 = bf16[784,4,512]{2,1,0:T(4,128)(2,1)} custom-call(bf16[4,3136,128]{2,1,0:T(8,128)(2,1)S(1)} %get-tuple-element.8.x_ref, f32[4,3136,128]{2,1,0:T(8,128)S(1)} %get-tuple-element.9.z3_ref, f32[2,256]{1,0:T(2,128)S(1)} %get-tuple-element.10.coef_ref), custom_call_target="tpu_custom_call" | custom-call | tf_op jit(solution)/shard_map/finish/pallas_call | solution.py:462

commit v5 on v4

--- a/solution.py
+++ b/solution.py
@@ -17,13 +17,12 @@
 
 
 def coefficients(total, gain, bias, run_var, count):
-    mean_offset = total[0:1] / count
-    variance = jnp.maximum(total[1:2] / count - mean_offset * mean_offset, 0.0)
-    sigma = jnp.sqrt(variance + epsilon)
-    run_sigma = jnp.sqrt(run_var + epsilon)
-    ratio = jnp.clip(sigma / run_sigma, 1.0 / ratio_max, ratio_max)
-    shift = jnp.clip(mean_offset / run_sigma, -shift_max, shift_max)
-    scale = gain * (ratio / sigma)
+    mean_offset = total[0:1] * (1.0 / count)
+    variance = jnp.maximum(total[1:2] * (1.0 / count) - mean_offset * mean_offset, 0.0)
+    inverse = lax.rsqrt(variance + epsilon)
+    run_inverse = lax.rsqrt(run_var + epsilon)
+    scale = gain * jnp.clip(run_inverse, inverse * (1.0 / ratio_max), inverse * ratio_max)
+    shift = jnp.clip(mean_offset * run_inverse, -shift_max, shift_max)
     return scale, gain * shift + bias - mean_offset * scale
 
 
@@ -370,7 +369,7 @@
             lax.fori_loop(0, total_rows // chunk, keep, 0)
 
 
-def last_kernel(pieces, x_ref, z3_ref, coef_ref, o_ref, y_ref, out_sem, old_sem):
+def last_kernel(pieces, x_ref, z3_ref, coef_ref, o_ref, y_ref, out_sem):
     slabs = x_ref.shape[0]
     pixels, images, channels = o_ref.shape
     part = pixels // pieces * images
@@ -380,13 +379,13 @@
 
     def old_copy(c):
         return pltpu.make_async_copy(
-            x_ref.at[c], flat_ref.at[:, pl.ds(c * LANES, LANES)], old_sem.at[c]
+            x_ref.at[c], flat_ref.at[:, pl.ds(c * LANES, LANES)], out_sem.at[0]
         )
 
     def slab_copy(t, c):
         span = pl.ds(t * part, part)
         far = flat_ref.at[span, pl.ds((done + c) * LANES, LANES)]
-        return pltpu.make_async_copy(y_ref.at[c, span], far, out_sem.at[t, c])
+        return pltpu.make_async_copy(y_ref.at[c, span], far, out_sem.at[1])
 
     for c in range(done):
         old_copy(c).start()
@@ -403,11 +402,10 @@
         return carry
 
     lax.fori_loop(0, pieces, step, 0)
-    for c in range(done):
-        old_copy(c).wait()
-    for t in range(pieces):
-        for c in range(per):
-            slab_copy(t, c).wait()
+    if done:
+        old = x_ref.at[pl.ds(0, done)]
+        pltpu.make_async_copy(old, old, out_sem.at[0]).wait()
+    pltpu.make_async_copy(y_ref, y_ref, out_sem.at[1]).wait()
 
 
 def local(mesh_rows, mesh_cols, images, w_reduce, w_spatial, w_expand, *params):
@@ -466,8 +464,7 @@
         out_specs=anywhere,
         scratch_shapes=[
             pltpu.VMEM((width // LANES, pixels * held, LANES), bf16),
-            pltpu.SemaphoreType.DMA((pieces, width // LANES)),
-            pltpu.SemaphoreType.DMA((slabs,)),
+            pltpu.SemaphoreType.DMA((2,)),
         ],
         compiler_params=pltpu.CompilerParams(vmem_limit_bytes=16 * 1024 * 1024),
         name="finish",

time: 43.5 us -> 43.3 us (level)
  no operation moved by 1% of the time
where the time goes in v5:
time: 43.3 us; the launch traced here: 43.2 us
  Pallas kernels  43.2 us (100%)
    pallas_call x1, Pallas kernels, local(): pl.pallas_call(functools.partial(main_kernel, mesh_rows, mesh_cols, count...  41.5 us
    pallas_call x1, Pallas kernels, local(): pl.pallas_call(functools.partial(last_kernel, pieces), out_shape=jax.Shap...  1.68 us

profile of v5, /device:TPU:0, one launch (start us, length us, event | category | flops | bytes accessed | tf_op | source)
XLA Modules:
  0.0 43.2 jit_solution(1871141260901742831)
XLA Ops:
  0.0 41.5 %bottlenecks.1 = (bf16[4,3136,128]{2,1,0:T(8,128)(2,1)S(1)}, f32[4,3136,128]{2,1,0:T(8,128)S(1)}, f32[2,256]{1,0:T(2,128)S(1)}) custom-call(bf16[784,4,512]{2,1,0:T(4,128)(2,1)} %bitcast.7, bf16[2,512,128]{2,1,0:T(8,128)(2,1)} %wr_hbm.1, bf16[2,1152,128]{2,1,0:T(8,128)(2,1)} %bitcast.8, bf16[2,128,512]{2,1,0:T(8,128)(2,1)} %we_hbm.1, f32[2,2,128]{2,1,0:T(2,128)} %gm_hbm.1, ...), custom_call_target="tpu_custom_call" | custom-call | tf_op jit(solution)/shard_map/bottlenecks/pallas_call | solution.py:430
  41.5 1.7 %finish.1 = bf16[784,4,512]{2,1,0:T(4,128)(2,1)} custom-call(bf16[4,3136,128]{2,1,0:T(8,128)(2,1)S(1)} %get-tuple-element.8.x_ref, f32[4,3136,128]{2,1,0:T(8,128)S(1)} %get-tuple-element.9.z3_ref, f32[2,256]{1,0:T(2,128)S(1)} %get-tuple-element.10.coef_ref), custom_call_target="tpu_custom_call" | custom-call | tf_op jit(solution)/shard_map/finish/pallas_call | solution.py:460

commit v6 on v5

--- a/solution.py
+++ b/solution.py
@@ -203,11 +203,11 @@
         return jnp.sum(ref[...], axis=0)
 
     def moments(d, sums):
-        d = d.reshape(-1, 16, d.shape[-1])
+        d = d.reshape(-1, 8, d.shape[-1])
         return sums[0] + jnp.sum(d, axis=0), sums[1] + jnp.sum(d * d, axis=0)
 
     def zeros(c):
-        return (jnp.zeros((16, c), f32), jnp.zeros((16, c), f32))
+        return (jnp.zeros((8, c), f32), jnp.zeros((8, c), f32))
 
     for copy in loads[:2]:
         copy.wait()

time: 43.3 us -> 43.3 us (level)
  no operation moved by 1% of the time
where the time goes in v6:
time: 43.3 us; the launch traced here: 43.2 us
  Pallas kernels  43.2 us (100%)
    pallas_call x1, Pallas kernels, local(): pl.pallas_call(functools.partial(main_kernel, mesh_rows, mesh_cols, count...  41.5 us
    pallas_call x1, Pallas kernels, local(): pl.pallas_call(functools.partial(last_kernel, pieces), out_shape=jax.Shap...  1.68 us

profile of v6, /device:TPU:0, one launch (start us, length us, event | category | flops | bytes accessed | tf_op | source)
XLA Modules:
  0.0 43.2 jit_solution(11091318840753279367)
XLA Ops:
  0.0 41.5 %bottlenecks.1 = (bf16[4,3136,128]{2,1,0:T(8,128)(2,1)S(1)}, f32[4,3136,128]{2,1,0:T(8,128)S(1)}, f32[2,256]{1,0:T(2,128)S(1)}) custom-call(bf16[784,4,512]{2,1,0:T(4,128)(2,1)} %bitcast.7, bf16[2,512,128]{2,1,0:T(8,128)(2,1)} %wr_hbm.1, bf16[2,1152,128]{2,1,0:T(8,128)(2,1)} %bitcast.8, bf16[2,128,512]{2,1,0:T(8,128)(2,1)} %we_hbm.1, f32[2,2,128]{2,1,0:T(2,128)} %gm_hbm.1, ...), custom_call_target="tpu_custom_call" | custom-call | tf_op jit(solution)/shard_map/bottlenecks/pallas_call | solution.py:430
  41.5 1.7 %finish.1 = bf16[784,4,512]{2,1,0:T(4,128)(2,1)} custom-call(bf16[4,3136,128]{2,1,0:T(8,128)(2,1)S(1)} %get-tuple-element.8.x_ref, f32[4,3136,128]{2,1,0:T(8,128)S(1)} %get-tuple-element.9.z3_ref, f32[2,256]{1,0:T(2,128)S(1)} %get-tuple-element.10.coef_ref), custom_call_target="tpu_custom_call" | custom-call | tf_op jit(solution)/shard_map/finish/pallas_call | solution.py:460
